TPU v7x, 32 devices: a whole 2x2x4 slice. The times are simulated.
32 devices in a mesh: row: 4 (over y, x), col: 8 (over z, core).
Axes of the slice: x: 2, y: 2, z: 4, core: 2. Of those that a mesh axis runs over, the one named last changes fastest.
Arguments:
- view_a: bfloat16 [3072, 8192], P(('row', 'col')), may hold values from -1000 to 1000
- view_b: bfloat16 [3072, 8192], P(('row', 'col')), may hold values from -1000 to 1000
Outputs:
- correlation: float32 [8192, 8192], P('row', 'col')
- loss: float32 [], replicated
All inputs are finite; a program needn't handle non-finite values.
Results may differ from a plain program's by a relative error of at most 0.0013.
Values may be sent and summed in bfloat16 or wider, within the bound.
A program may use at most 192 MiB of HBM per device.

v0:
```python
import jax
import jax.numpy as jnp
from jax import lax
from jax.sharding import PartitionSpec as P


def moments(view):
    values = view.astype(jnp.float32)
    return (jnp.sum(values, 0), jnp.sum(values * values, 0))


def scaled(view, total, squares, count):
    mean = total / count
    var = squares / count - mean * mean
    return ((view.astype(jnp.float32) - mean) * lax.rsqrt(var + 1e-05)).astype(jnp.bfloat16)


def shards(view_a, view_b):
    rows_local = view_a.shape[0]
    width = view_a.shape[1]
    n_row = lax.axis_size("row")
    n_col = lax.axis_size("col")
    count = rows_local * n_row * n_col
    left = lax.all_to_all(view_a, "row", split_axis=1, concat_axis=0, tiled=True)
    right = lax.all_to_all(view_b, "col", split_axis=1, concat_axis=0, tiled=True)
    part_total, part_squares = moments(left)
    part_total, part_squares = lax.psum((part_total, part_squares), "col")
    left = scaled(left, part_total, part_squares, count)
    side_total, side_squares = moments(right)
    side_total, side_squares = lax.psum((side_total, side_squares), "row")
    right = scaled(right, side_total, side_squares, count)
    row_block = left.shape[1]
    col_block = right.shape[1]
    every_left = lax.all_gather(left, "col", axis=0, tiled=True)
    grouped = every_left.reshape(n_col, n_row, rows_local, row_block)
    piece = lax.all_gather(right, "row", axis=0, tiled=True)
    groups = piece.shape[0] // right.shape[0]
    blocks = piece.reshape(groups, n_col, rows_local, col_block)
    product = jnp.einsum("ckbf,kcbg->fg", grouped, blocks, preferred_element_type=jnp.float32)
    correlation = product / count
    row_ids = lax.axis_index("row") * row_block + lax.broadcasted_iota(jnp.int32, (row_block, 1), 0)
    col_ids = lax.axis_index("col") * col_block + lax.broadcasted_iota(jnp.int32, (1, col_block), 1)
    on_diag = row_ids == col_ids
    squared = correlation * correlation
    diag_terms = jnp.where(on_diag, (1.0 - correlation) ** 2 - 0.0051 * squared, 0.0)
    partial_loss = 0.0051 * jnp.sum(squared) + jnp.sum(diag_terms)
    loss = lax.psum(partial_loss, ("row", "col")) / width
    return (correlation, loss)


def solution(mesh):
    return jax.shard_map(
        shards,
        mesh=mesh,
        in_specs=(P(("row", "col"), None), P(("row", "col"), None)),
        out_specs=(P("row", "col"), P()),
        check_vma=False,
    )
```

profile of v0, /device:TPU:12, one launch (start us, length us, event | category | flops | bytes accessed | tf_op | source)
XLA Modules:
  0.0 330.5 jit_solution(2563064573535867003)
XLA Ops:
  7.2 0.0 all-gather.5.cloned.1.call-start
  7.2 1.5 copy.26
  8.8 40.6 %all_to_all.26 = bf16[96,8,1024]{2,0,1:T(8,128)(2,1)S(1)} all-to-all(bf16[96,8,1024]{2,0,1:T(8,128)(2,1)S(1)} %bitcast.31), channel_id=1, replica_groups=mesh['row'=4,'col'=8] {'col'}, dimensions={1} | all-to-all | bytes 3145728 | tf_op jit(solution)/shard_map/all_to_all | solution.py:25
  49.4 0.0 copy-start
  49.4 0.5 convert_reduce_fusion
  49.8 9.1 %all-reduce.1 = (f32[1024]{0:T(1024)S(1)}, f32[1024]{0:T(1024)S(1)}) all-reduce(f32[1024]{0:T(1024)S(1)} %get-tuple-element.5, f32[1024]{0:T(1024)S(1)} %get-tuple-element.4), channel_id=1, replica_groups=mesh['row'=4,'col'=8] {'row'}, use_global_device_ids=true, to_apply=%region_7.0 | all-reduce | flops 2048 | bytes 16384 | tf_op jit(solution)/shard_map/psum | solution.py:30
  59.0 1.6 fusion.5
  60.6 0.0 all-gather.5.cloned.1.call-update
  60.6 0.0 all-gather.3.cloned.1.call-start
  60.7 0.0 copy-done
  60.7 0.2 copy.27
  60.8 33.6 %all_to_all.27 = bf16[96,4,2048]{2,0,1:T(8,128)(2,1)S(1)} all-to-all(bf16[96,4,2048]{2,0,1:T(8,128)(2,1)S(1)} %bitcast.32), channel_id=1, replica_groups=mesh['row'=4,'col'=8] {'row'}, dimensions={1} | all-to-all | bytes 3145728 | tf_op jit(solution)/shard_map/all_to_all | solution.py:24
  94.4 0.4 convert_reduce_fusion.1
  94.9 26.0 %all-reduce = (f32[2048]{0:T(1024)S(1)}, f32[2048]{0:T(1024)S(1)}) all-reduce(f32[2048]{0:T(1024)S(1)} %get-tuple-element.7, f32[2048]{0:T(1024)S(1)} %get-tuple-element.6), channel_id=1, replica_groups=mesh['row'=4,'col'=8] {'col'}, use_global_device_ids=true, to_apply=%region_3.0 | all-reduce | flops 4096 | bytes 32768 | tf_op jit(solution)/shard_map/psum | solution.py:27
  120.9 1.6 fusion.7
  122.4 0.0 all-gather.3.cloned.1.call-update
  122.5 17.6 %all-gather.5.cloned.1.call-done = bf16[3072,1024]{1,0:T(8,128)(2,1)} async-done(((bf16[768,1024]{1,0:T(8,128)(2,1)}), bf16[3072,1024]{1,0:T(8,128)(2,1)}) %all-gather.5.cloned.1.call-update) | async-done | bytes 6291472 | tf_op jit(solution)/shard_map/all_gather | solution.py:36
  140.1 116.2 %all-gather.3.cloned.1.call-done = bf16[3072,2048]{1,0:T(8,128)(2,1)} async-done(((bf16[384,2048]{1,0:T(8,128)(2,1)}), bf16[3072,2048]{1,0:T(8,128)(2,1)}) %all-gather.3.cloned.1.call-update) | async-done | bytes 12582928 | tf_op jit(solution)/shard_map/all_gather | solution.py:34
  256.3 21.4 %select_reduce_fusion = (f32[]{:T(128)}, f32[]{:T(128)}, f32[2048,1024]{1,0:T(8,128)}) fusion(s32[1024]{0:T(1024)S(1)} %iota_add_fusion.1, s32[2048]{0:T(1024)S(1)} %iota_add_fusion, bf16[8,4,96,2048]{3,2,1,0:T(8,128)(2,1)} %bitcast.35, bf16[4,8,96,1024]{3,2,1,0:T(8,128)(2,1)} %bitcast.36), kind=kOutput, calls=%fused_computation.1 | convolution fusion | flops 12905873408 | bytes 27275272 | tf_op jit(solution)/shard_map/ckbf,kcbg->fg/dot_general | solution.py:39
  279.0 43.0 %psum.39 = f32[]{:T(128)} all-reduce(f32[]{:T(128)S(6)} %add.55), channel_id=1, replica_groups=mesh['row'=4,'col'=8] {'row','col'}, use_global_device_ids=true, to_apply=%region_10.11 | all-reduce | flops 1 | bytes 8 | tf_op jit(solution)/shard_map/psum | solution.py:47
  (4 shorter events, 0.0 us)
Async XLA Ops:
  7.2 132.9 %all-gather.5.cloned.1.call-start = ((), (), s32[]{:S(2)}) async-start(), calls=%async_computation.3 | async-start | bytes 7864320 | tf_op jit(solution)/shard_map/all_gather | solution.py:36
  49.4 11.3 %copy-start = (bf16[96,8192]{1,0:T(8,128)(2,1)S(1)}, bf16[96,8192]{1,0:T(8,128)(2,1)}, u32[]{:S(2)}) copy-start(bf16[96,8192]{1,0:T(8,128)(2,1)} %param.2) | copy-start | bytes 4718596
  60.6 195.7 %all-gather.3.cloned.1.call-start = ((), (), s32[]{:S(2)}) async-start(), calls=%async_computation.2 | async-start | bytes 14155776 | tf_op jit(solution)/shard_map/all_gather | solution.py:34
Sparse Core Ops, SparseCore 0:
  60.7 79.2 all-gather.4
  142.3 113.9 all-gather.2
where the time goes:
time: 331 us
  blocking collectives  152 us (46%)
  waiting for transfers between devices  134 us (40%)
  matrix products  21.4 us (6%)
  between operations  17.1 us (5%)
  other arithmetic  4.09 us (1%)
    all_gather x1, waiting for transfers between devices, shards(): every_left = lax.all_gather(left, 'col', axis=0, tiled=True)  116 us
    psum x1, blocking collectives, shards(): loss = lax.psum(partial_loss, ('row', 'col')) / width  43 us
    all_to_all x1, blocking collectives, shards(): lax.all_to_all(view_b, 'col', split_axis=1, concat_axis=0, tiled=True)  40.6 us
    all_to_all x1, blocking collectives, shards(): lax.all_to_all(view_a, 'row', split_axis=1, concat_axis=0, tiled=True)  33.6 us
    psum x1, blocking collectives, shards(): part_total, part_squares = lax.psum((part_total, part_squares), 'col')  26 us
    dot_general x1, matrix products, shards(): jnp.einsum('ckbf,kcbg->fg', grouped, blocks, preferred_element_type=jnp.f...  21.4 us
    all_gather x1, waiting for transfers between devices, shards(): piece = lax.all_gather(right, 'row', axis=0, tiled=True)  17.6 us
    psum x1, blocking collectives, shards(): side_total, side_squares = lax.psum((side_total, side_squares), 'row')  9.11 us
  transfers between devices with their start and end apart: 2, of which 2 were waited for; matrix products, arithmetic and copies ran while one was open for 1% of the time, Pallas kernels for 0%

commit v1 on v0

--- a/solution.py
+++ b/solution.py
@@ -2,6 +2,13 @@
 import jax.numpy as jnp
 from jax import lax
 from jax.sharding import PartitionSpec as P
+
+
+def swap_blocks(x, axis, split, join):
+    n_dev = lax.axis_size(axis)
+    blocks = jnp.stack(jnp.split(x, n_dev, axis=split), axis=0)
+    blocks = lax.all_to_all(blocks, axis, split_axis=0, concat_axis=0)
+    return jnp.concatenate(blocks, axis=join)
 
 
 def moments(view):
@@ -21,7 +28,7 @@
     n_row = lax.axis_size("row")
     n_col = lax.axis_size("col")
     count = rows_local * n_row * n_col
-    left = lax.all_to_all(view_a, "row", split_axis=1, concat_axis=0, tiled=True)
+    left = swap_blocks(view_a, "row", 1, 0)
     right = lax.all_to_all(view_b, "col", split_axis=1, concat_axis=0, tiled=True)
     part_total, part_squares = moments(left)
     part_total, part_squares = lax.psum((part_total, part_squares), "col")

time: 331 us -> 331 us (level)
  no operation moved by 1% of the time
where the time goes in v1:
time: 331 us
  blocking collectives  152 us (46%)
  waiting for transfers between devices  134 us (40%)
  matrix products  21.4 us (6%)
  between operations  17.2 us (5%)
  other arithmetic  4.33 us (1%)
    all_gather x1, waiting for transfers between devices, shards(): every_left = lax.all_gather(left, 'col', axis=0, tiled=True)  116 us
    psum x1, blocking collectives, shards(): loss = lax.psum(partial_loss, ('row', 'col')) / width  43 us
    all_to_all x1, blocking collectives, shards(): lax.all_to_all(view_b, 'col', split_axis=1, concat_axis=0, tiled=True)  40.6 us
    all_to_all x1, blocking collectives, swap_blocks(): blocks = lax.all_to_all(blocks, axis, split_axis=0, concat_axis=0)  33.7 us
    psum x1, blocking collectives, shards(): part_total, part_squares = lax.psum((part_total, part_squares), 'col')  26 us
    dot_general x1, matrix products, shards(): jnp.einsum('ckbf,kcbg->fg', grouped, blocks, preferred_element_type=jnp.f...  21.4 us
    all_gather x1, waiting for transfers between devices, shards(): piece = lax.all_gather(right, 'row', axis=0, tiled=True)  17.4 us
    psum x1, blocking collectives, shards(): side_total, side_squares = lax.psum((side_total, side_squares), 'row')  9.11 us
  transfers between devices with their start and end apart: 2, of which 2 were waited for; matrix products, arithmetic and copies ran while one was open for 1% of the time, Pallas kernels for 0%

profile of v1, /device:TPU:12, one launch (start us, length us, event | category | flops | bytes accessed | tf_op | source)
XLA Modules:
  0.0 330.7 jit_solution(7954161227893274463)
XLA Ops:
  7.2 0.0 all-gather.5.cloned.1.call-start
  7.2 1.6 copy.18
  8.8 40.6 %all_to_all.18 = bf16[96,8,1024]{2,0,1:T(8,128)(2,1)S(1)} all-to-all(bf16[96,8,1024]{2,0,1:T(8,128)(2,1)S(1)} %bitcast.33), channel_id=1, replica_groups=mesh['row'=4,'col'=8] {'col'}, dimensions={1} | all-to-all | bytes 3145728 | tf_op jit(solution)/shard_map/all_to_all | solution.py:32
  49.4 0.0 copy-start
  49.4 0.5 convert_reduce_fusion
  49.9 9.1 %all-reduce.1 = (f32[1024]{0:T(1024)S(1)}, f32[1024]{0:T(1024)S(1)}) all-reduce(f32[1024]{0:T(1024)S(1)} %get-tuple-element.5, f32[1024]{0:T(1024)S(1)} %get-tuple-element.4), channel_id=1, replica_groups=mesh['row'=4,'col'=8] {'row'}, use_global_device_ids=true, to_apply=%region_7.0 | all-reduce | flops 2048 | bytes 16384 | tf_op jit(solution)/shard_map/psum | solution.py:37
  59.0 1.6 fusion.5
  60.6 0.0 all-gather.5.cloned.1.call-update
  60.6 0.0 all-gather.3.cloned.1.call-start
  60.7 0.0 copy-done
  60.7 0.1 slice_bitcast_fusion.3
  60.8 0.2 pad_maximum_fusion
  61.0 33.7 %all_to_all.19 = bf16[4,96,2048]{2,1,0:T(8,128)(2,1)S(1)} all-to-all(bf16[4,96,2048]{2,1,0:T(8,128)(2,1)S(1)} %pad_maximum_fusion), channel_id=1, replica_groups=mesh['row'=4,'col'=8] {'row'}, dimensions={0} | all-to-all | bytes 3145728 | tf_op jit(solution)/shard_map/all_to_all | solution.py:10
  94.7 0.4 convert_reduce_fusion.1
  95.2 26.0 %all-reduce = (f32[2048]{0:T(1024)S(1)}, f32[2048]{0:T(1024)S(1)}) all-reduce(f32[2048]{0:T(1024)S(1)} %get-tuple-element.7, f32[2048]{0:T(1024)S(1)} %get-tuple-element.6), channel_id=1, replica_groups=mesh['row'=4,'col'=8] {'col'}, use_global_device_ids=true, to_apply=%region_3.0 | all-reduce | flops 4096 | bytes 32768 | tf_op jit(solution)/shard_map/psum | solution.py:34
  121.2 1.6 fusion.7
  122.8 0.0 all-gather.3.cloned.1.call-update
  122.8 17.4 %all-gather.5.cloned.1.call-done = bf16[3072,1024]{1,0:T(8,128)(2,1)} async-done(((bf16[768,1024]{1,0:T(8,128)(2,1)}), bf16[3072,1024]{1,0:T(8,128)(2,1)}) %all-gather.5.cloned.1.call-update) | async-done | bytes 6291472 | tf_op jit(solution)/shard_map/all_gather | solution.py:43
  140.2 116.2 %all-gather.3.cloned.1.call-done = bf16[3072,2048]{1,0:T(8,128)(2,1)} async-done(((bf16[384,2048]{1,0:T(8,128)(2,1)}), bf16[3072,2048]{1,0:T(8,128)(2,1)}) %all-gather.3.cloned.1.call-update) | async-done | bytes 12582928 | tf_op jit(solution)/shard_map/all_gather | solution.py:41
  256.4 21.4 %select_reduce_fusion = (f32[]{:T(128)}, f32[]{:T(128)}, f32[2048,1024]{1,0:T(8,128)}) fusion(s32[1024]{0:T(1024)S(1)} %iota_add_fusion.1, s32[2048]{0:T(1024)S(1)} %iota_add_fusion, bf16[8,4,96,2048]{3,2,1,0:T(8,128)(2,1)} %bitcast.35, bf16[4,8,96,1024]{3,2,1,0:T(8,128)(2,1)} %bitcast.36), kind=kOutput, calls=%fused_computation.1 | convolution fusion | flops 12905873408 | bytes 27275272 | tf_op jit(solution)/shard_map/ckbf,kcbg->fg/dot_general | solution.py:46
  279.1 43.0 %psum.39 = f32[]{:T(128)} all-reduce(f32[]{:T(128)S(6)} %add.55), channel_id=1, replica_groups=mesh['row'=4,'col'=8] {'row','col'}, use_global_device_ids=true, to_apply=%region_10.11 | all-reduce | flops 1 | bytes 8 | tf_op jit(solution)/shard_map/psum | solution.py:54
  (4 shorter events, 0.0 us)
Async XLA Ops:
  7.2 133.1 %all-gather.5.cloned.1.call-start = ((), (), s32[]{:S(2)}) async-start(), calls=%async_computation.3 | async-start | bytes 7864320 | tf_op jit(solution)/shard_map/all_gather | solution.py:43
  49.4 11.3 %copy-start = (bf16[96,8192]{1,0:T(8,128)(2,1)S(1)}, bf16[96,8192]{1,0:T(8,128)(2,1)}, u32[]{:S(2)}) copy-start(bf16[96,8192]{1,0:T(8,128)(2,1)} %param.2) | copy-start | bytes 4718596
  60.6 195.8 %all-gather.3.cloned.1.call-start = ((), (), s32[]{:S(2)}) async-start(), calls=%async_computation.2 | async-start | bytes 14155776 | tf_op jit(solution)/shard_map/all_gather | solution.py:41
Sparse Core Ops, SparseCore 0:
  60.7 79.4 all-gather.4
  142.4 113.9 all-gather.2
